TPU v7x, 32 devices: a whole 2x2x4 slice. The times are simulated.
32 devices in a mesh: owner: 4 (over y, x), rows: 8 (over z, core).
Axes of the slice: x: 2, y: 2, z: 4, core: 2. Of those that a mesh axis runs over, the one named last changes fastest.
Arguments:
- train_gate: float32 [64, 2048, 1024], P('owner', 'rows'), may hold values from -0.1875 to 0.1875
- train_up: float32 [64, 2048, 1024], P('owner', 'rows'), may hold values from -0.1875 to 0.1875
- train_down: float32 [64, 1024, 2048], P('owner', None, 'rows'), may hold values from -0.25 to 0.25
- router_weight: float32 [2048, 64], P('rows', 'owner'), may hold values from -0.125 to 0.125
- router_gain: float32 [2048], P('rows'), may hold values from 0.25 to 1.75
Outputs:
- ready_gate: bfloat16 [64, 2048, 1024], P('owner', None, 'rows')
- ready_up: bfloat16 [64, 2048, 1024], P('owner', None, 'rows')
- ready_down: bfloat16 [64, 1024, 2048], P('owner', 'rows')
- scale_gate: float32 [64, 1024], P('owner', 'rows')
- scale_up: float32 [64, 1024], P('owner', 'rows')
- scale_down: float32 [64, 1024], P('owner', 'rows')
- serve_router: bfloat16 [2048, 64], replicated
All inputs are finite; a program needn't handle non-finite values. Where the computation divides by a largest or mean magnitude, that divisor is 1e-20 or more.
Results may differ from a plain program's by a relative error of at most 0.0013.
Values may be sent and summed in bfloat16 or wider, within the bound.
A program may use at most 192 MiB of HBM per device.

v0:
```python
import jax
import jax.numpy as jnp
from jax import lax
from jax.sharding import PartitionSpec as P

D_MODEL = 2048


def local(train_gate, train_up, train_down, router_weight, router_gain):
    total_gate, total_up, total_down = lax.psum(
        (
            jnp.sum(jnp.abs(train_gate), axis=1),
            jnp.sum(jnp.abs(train_up), axis=1),
            jnp.sum(jnp.abs(train_down), axis=2),
        ),
        "rows",
    )
    scale_gate = total_gate / D_MODEL
    scale_up = total_up / D_MODEL
    scale_down = total_down / D_MODEL
    narrow_gate, narrow_up, narrow_down = (
        (train_gate / jnp.expand_dims(scale_gate, 1)).astype(jnp.bfloat16),
        (train_up / jnp.expand_dims(scale_up, 1)).astype(jnp.bfloat16),
        (train_down / jnp.expand_dims(scale_down, 2)).astype(jnp.bfloat16),
    )
    ready_gate, ready_up = (
        lax.all_to_all(narrow_gate, "rows", split_axis=2, concat_axis=1, tiled=True),
        lax.all_to_all(narrow_up, "rows", split_axis=2, concat_axis=1, tiled=True),
    )
    ready_down = lax.all_to_all(narrow_down, "rows", split_axis=1, concat_axis=2, tiled=True)
    scale_gate = lax.dynamic_slice_in_dim(
        scale_gate, lax.axis_index("rows") * ready_gate.shape[2], ready_gate.shape[2], axis=1
    )
    scale_up = lax.dynamic_slice_in_dim(
        scale_up, lax.axis_index("rows") * ready_up.shape[2], ready_up.shape[2], axis=1
    )
    scale_down = lax.dynamic_slice_in_dim(
        scale_down, lax.axis_index("rows") * ready_down.shape[1], ready_down.shape[1], axis=1
    )
    part_router = (router_weight * router_gain[:, None]).astype(jnp.bfloat16)
    row_router = lax.all_gather(part_router, "rows", axis=0, tiled=True)
    serve_router = lax.all_gather(row_router, "owner", axis=1, tiled=True)
    return (ready_gate, ready_up, ready_down, scale_gate, scale_up, scale_down, serve_router)


def solution(mesh):
    return jax.shard_map(
        local,
        mesh=mesh,
        in_specs=(
            P("owner", "rows", None),
            P("owner", "rows", None),
            P("owner", None, "rows"),
            P("rows", "owner"),
            P("rows"),
        ),
        out_specs=(
            P("owner", None, "rows"),
            P("owner", None, "rows"),
            P("owner", "rows", None),
            P("owner", "rows"),
            P("owner", "rows"),
            P("owner", "rows"),
            P(),
        ),
        check_vma=False,
    )
```

profile of v0, /device:TPU:0, one launch (start us, length us, event | category | flops | bytes accessed | tf_op | source)
XLA Modules:
  0.0 737.8 jit_solution(7608499507201470121)
XLA Ops:
  7.2 0.0 all-reduce.3.cloned.1.call-start
  7.2 8.6 %abs_reduce_fusion = f32[16,1024]{1,0:T(8,128)} fusion(f32[16,1024,256]{2,1,0:T(8,128)} %param.7), kind=kLoop, calls=%fused_computation.2 | loop fusion | flops 8372224 | bytes 16842752 | tf_op jit(solution)/shard_map/reduce_sum | solution.py:14
  15.8 12.6 %abs_reduce_fusion.1 = (f32[16,1024]{1,0:T(8,128)}, f32[16,1024]{1,0:T(8,128)}) fusion(f32[16,256,1024]{2,1,0:T(8,128)} %param.6, f32[16,256,1024]{2,1,0:T(8,128)} %param.5), kind=kLoop, calls=%fused_computation.4 | loop fusion | flops 16744448 | bytes 33685504 | tf_op jit(solution)/shard_map/reduce_sum | solution.py:13
  28.4 0.0 all-reduce.3.cloned.1.call-update
  28.4 17.6 %copy.19 = f32[16,256,1024]{1,0,2:T(8,128)} copy(f32[16,256,1024]{2,1,0:T(8,128)} %param.6) | data formatting | bytes 33554432 | tf_op args[1]
  46.1 40.7 %all-reduce.3.cloned.1.call-done = (f32[16,1024]{1,0:T(8,128)}, f32[16,1024]{1,0:T(8,128)}, f32[16,1024]{1,0:T(8,128)}) async-done(((f32[16,1024]{1,0:T(8,128)}, f32[16,1024]{1,0:T(8,128)}, f32[16,1024]{1,0:T(8,128)}), (f32[16,1024]{1,0:T(8,128)}, f32[16,1024]{1,0:T(8,128)}, f32[16,1024]{1,0:T(8,128)})) %all-reduce.3.cloned.1.call-update) | async-done | bytes 196624 | tf_op jit(solution)/shard_map/psum | solution.py:10
  86.8 0.8 broadcast_multiply_fusion.1
  87.6 0.2 copy.18
  87.8 9.6 %divide_convert_fusion = bf16[16,256,1024]{1,0,2:T(8,128)(2,1)} fusion(f32[16,256,1024]{1,0,2:T(8,128)} %copy.19, f32[16,1024]{0,1:T(8,128)S(1)} %copy.18), kind=kLoop, calls=%fused_computation.3 | loop fusion | flops 8388608 | bytes 25231360 | tf_op jit(solution)/shard_map/convert_element_type | solution.py:23
  97.5 4.9 all-to-all-start.1
  102.4 17.6 %copy.16 = f32[16,256,1024]{1,0,2:T(8,128)} copy(f32[16,256,1024]{2,1,0:T(8,128)} %param.5) | data formatting | bytes 33554432 | tf_op args[0]
  120.0 0.2 copy.15
  120.3 9.7 %divide_convert_fusion.1 = bf16[16,256,1024]{1,0,2:T(8,128)(2,1)} fusion(f32[16,256,1024]{1,0,2:T(8,128)} %copy.16, f32[16,1024]{0,1:T(8,128)S(1)} %copy.15), kind=kLoop, calls=%fused_computation.5 | loop fusion | flops 8388608 | bytes 25231360 | tf_op jit(solution)/shard_map/convert_element_type | solution.py:22
  129.9 156.3 %all-to-all-done.1 = bf16[16,256,1024]{1,0,2:T(8,128)(2,1)} async-done(((bf16[16,256,1024]{1,0,2:T(8,128)(2,1)}), bf16[16,256,1024]{1,0,2:T(8,128)(2,1)}, u32[]{:S(2)}, u32[]{:S(2)}) %all-to-all-start.1) | async-done | bytes 8388640 | tf_op jit(solution)/shard_map/all_to_all | solution.py:28
  286.3 4.9 all-to-all-start
  291.2 0.2 copy.21
  291.4 0.0 copy-start.2
  291.4 0.0 copy-start.3
  291.5 16.6 %fusion = bf16[16,1024,256]{2,0,1:T(8,128)(2,1)} fusion(f32[16,1024,256]{2,1,0:T(8,128)} %param.7, f32[16,1024]{0,1:T(8,128)S(1)} %copy.21), kind=kLoop, calls=%fused_computation.1 | loop fusion | flops 8388608 | bytes 25231360 | tf_op jit(solution)/shard_map/convert_element_type | solution.py:24
  308.1 167.0 %all-to-all-done = bf16[16,256,1024]{1,0,2:T(8,128)(2,1)} async-done(((bf16[16,256,1024]{1,0,2:T(8,128)(2,1)}), bf16[16,256,1024]{1,0,2:T(8,128)(2,1)}, u32[]{:S(2)}, u32[]{:S(2)}) %all-to-all-start) | async-done | bytes 8388640 | tf_op jit(solution)/shard_map/all_to_all | solution.py:27
  475.1 5.0 all-to-all-start.2
  480.1 189.9 %all_gather.6 = bf16[2048,16]{0,1:T(8,128)(2,1)S(1)} all-gather(bf16[256,16]{0,1:T(8,128)(2,1)S(1)} %multiply_convert_fusion), channel_id=1, replica_groups=mesh['owner'=4,'rows'=8] {'rows'}, dimensions={0}, use_global_device_ids=true | all-gather | bytes 73728 | tf_op jit(solution)/shard_map/all_gather | solution.py:41
  670.0 9.1 %all_gather.7 = bf16[2048,64]{0,1:T(8,128)(2,1)S(1)} all-gather(bf16[2048,16]{0,1:T(8,128)(2,1)S(1)} %all_gather.6), channel_id=1, replica_groups=mesh['owner'=4,'rows'=8] {'owner'}, dimensions={1}, use_global_device_ids=true | all-gather | bytes 327680 | tf_op jit(solution)/shard_map/all_gather | solution.py:42
  679.1 0.6 constant_dynamic-slice_fusion
  679.7 0.6 constant_dynamic-slice_fusion.1
  680.3 0.6 constant_dynamic-slice_fusion.2
  680.9 12.3 %copy.20 = bf16[16,8,256,128]{3,2,1,0:T(8,128)(2,1)} copy(bf16[16,8,256,128]{2,0,3,1:T(8,128)(2,1)} %bitcast.4) | data formatting | bytes 16777216 | tf_op jit(solution)/shard_map/all_to_all | solution.py:28
  693.2 12.3 %copy.17 = bf16[16,8,256,128]{3,2,1,0:T(8,128)(2,1)} copy(bf16[16,8,256,128]{2,0,3,1:T(8,128)(2,1)} %bitcast.1) | data formatting | bytes 16777216 | tf_op jit(solution)/shard_map/all_to_all | solution.py:27
  705.5 0.0 all-to-all-done.2
  705.5 11.4 %copy.23 = bf16[16,128,8,256]{3,2,1,0:T(8,128)(2,1)} copy(bf16[16,128,8,256]{3,0,1,2:T(8,128)(2,1)} %bitcast.7) | data formatting | bytes 16777216 | tf_op jit(solution)/shard_map/all_to_all | solution.py:30
  716.9 13.4 %all_to_all.50 = bf16[16,128,2048]{2,1,0:T(8,128)(2,1)} reshape(bf16[16,128,8,256]{3,2,1,0:T(8,128)(2,1)} %copy.23) | data formatting | bytes 16777216 | tf_op jit(solution)/shard_map/all_to_all | solution.py:30
  730.3 0.7 copy.31
  (9 shorter events, 0.0 us)
Async XLA Ops:
  7.2 79.6 %all-reduce.3.cloned.1.call-start = ((), (), s32[]{:S(2)}) async-start(), calls=%async_computation.3 | async-start | bytes 393216 | tf_op jit(solution)/shard_map/psum | solution.py:10
  97.5 188.8 %all-to-all-start.1 = ((bf16[16,256,1024]{1,0,2:T(8,128)(2,1)}), bf16[16,256,1024]{1,0,2:T(8,128)(2,1)}, u32[]{:S(2)}, u32[]{:S(2)}) async-start(bf16[16,256,1024]{1,0,2:T(8,128)(2,1)} %divide_convert_fusion), calls=%async_computation.1 | async-start | bytes 16777216 | tf_op jit(solution)/shard_map/all_to_all | solution.py:28
  102.4 17.6 %copy-start.1 = (f32[16,1024]{1,0:T(8,128)S(1)}, f32[16,1024]{1,0:T(8,128)}, u32[]{:S(2)}) copy-start(f32[16,1024]{1,0:T(8,128)} %get-tuple-element.7) | copy-start | bytes 196612
  120.2 171.0 %copy-start = (f32[16,1024]{1,0:T(8,128)S(1)}, f32[16,1024]{1,0:T(8,128)}, u32[]{:S(2)}) copy-start(f32[16,1024]{1,0:T(8,128)} %get-tuple-element.9) | copy-start | bytes 196612
  286.3 188.8 %all-to-all-start = ((bf16[16,256,1024]{1,0,2:T(8,128)(2,1)}), bf16[16,256,1024]{1,0,2:T(8,128)(2,1)}, u32[]{:S(2)}, u32[]{:S(2)}) async-start(bf16[16,256,1024]{1,0,2:T(8,128)(2,1)} %divide_convert_fusion.1), calls=%async_computation | async-start | bytes 16777216 | tf_op jit(solution)/shard_map/all_to_all | solution.py:27
  291.4 188.7 %copy-start.2 = (f32[256,16]{0,1:T(8,128)S(1)}, f32[256,16]{0,1:T(8,128)}, u32[]{:S(2)}) copy-start(f32[256,16]{0,1:T(8,128)} %param.8) | copy-start | bytes 49156
  291.4 188.7 %copy-start.3 = (f32[256]{0:T(256)S(1)}, f32[256]{0:T(256)}, u32[]{:S(2)}) copy-start(f32[256]{0:T(256)} %param.9) | copy-start | bytes 3076
  475.1 230.4 %all-to-all-start.2 = ((bf16[16,1024,256]{2,0,1:T(8,128)(2,1)}), bf16[16,1024,256]{2,0,1:T(8,128)(2,1)}, u32[]{:S(2)}, u32[]{:S(2)}) async-start(bf16[16,1024,256]{2,0,1:T(8,128)(2,1)} %fusion), calls=%async_computation.2 | async-start | bytes 16777216 | tf_op jit(solution)/shard_map/all_to_all | solution.py:30
Sparse Core Ops, SparseCore 0:
  28.6 58.1 all-reduce.2
where the time goes:
time: 740 us; the launch traced here: 738 us
  waiting for transfers between devices  364 us (49%)
  blocking collectives  199 us (27%)
  local copies, waits for them, and re-layouts  87.7 us (12%)
  other arithmetic  58 us (8%)
  starting transfers between devices  14.9 us (2%)
  between operations  14.2 us (2%)
    all_gather x1, blocking collectives, local(): row_router = lax.all_gather(part_router, 'rows', axis=0, tiled=True)  190 us
    all_to_all x1, waiting for transfers between devices, local(): lax.all_to_all(narrow_gate, 'rows', split_axis=2, concat_axis=1, tiled=True)  167 us
    all_to_all x1, waiting for transfers between devices, local(): lax.all_to_all(narrow_up, 'rows', split_axis=2, concat_axis=1, tiled=True)  156 us
    psum x1, waiting for transfers between devices, local(): lax.psum((jnp.sum(jnp.abs(train_gate), axis=1), jnp.sum(jnp.abs(train_up)...  40.7 us
    unnamed x11, local copies, waits for them, and re-layouts  36 us
    all_to_all x2, local copies, waits for them, and re-layouts, local(): lax.all_to_all(narrow_down, 'rows', split_axis=1, concat_axis=2, tiled=True)  24.8 us
    convert_element_type x1, other arithmetic, local(): (train_down / jnp.expand_dims(scale_down, 2)).astype(jnp.bfloat16)  16.6 us
  transfers between devices with their start and end apart: 4, of which 3 were waited for; matrix products, arithmetic and copies ran while one was open for 12% of the time, Pallas kernels for 0%

commit v1 on v0

v1 whole, which is shorter than its diff:
```python
import functools

import jax
import jax.numpy as jnp
from jax import lax
from jax.experimental import pallas as pl
from jax.experimental.pallas import tpu as pltpu
from jax.sharding import PartitionSpec as P

CORES = 2
SLOTS = 4
GROUPS = 4
MESH = pl.DeviceIdType.MESH


def exchange(
    n,
    owners,
    gate,
    up,
    down,
    router,
    out_gate,
    out_up,
    out_down,
    out_scale,
    out_router,
    wide,
    tall,
    send_wide,
    send_tall,
    part,
    arrived,
    inverse,
    load_sem,
    own_sem,
    sum_send,
    sum_recv,
    inv_send,
    inv_recv,
    row_send,
    row_recv,
    col_send,
    col_recv,
    send_sem,
    recv_sem,
):
    me = lax.axis_index("rows")
    home = lax.axis_index("owner")
    experts, rows, _ = gate.shape
    share = out_gate.shape[2]
    slots = min(SLOTS, experts)
    per = max(1, experts // GROUPS)
    groups = experts // per
    chips = n // CORES
    chip = me // CORES
    core = lax.rem(me, CORES)

    def peer(k):
        return lax.rem(me + k, n)

    def remote(src, dst, out_sem, in_sem, **where):
        return pltpu.make_async_remote_copy(
            src_ref=src,
            dst_ref=dst,
            send_sem=out_sem,
            recv_sem=in_sem,
            device_id=where,
            device_id_type=MESH,
        )

    barrier = pltpu.get_barrier_semaphore()
    for k in range(1, n):
        pl.semaphore_signal(barrier, inc=1, device_id={"rows": peer(k)}, device_id_type=MESH)
    for k in range(1, owners):
        pl.semaphore_signal(
            barrier, inc=1, device_id={"owner": lax.rem(home + k, owners)}, device_id_type=MESH
        )

    def load(src, buf, e):
        slot = lax.rem(e, slots)
        kind = 0 if buf is wide else 1
        return pltpu.make_async_copy(src.at[e], buf.at[slot], load_sem.at[kind, slot])

    def fill(src, buf):
        for e in range(slots):
            load(src, buf, e).start()

    def take(src, buf, e, body):
        load(src, buf, e).wait()
        body(e, lax.rem(e, slots))

        @pl.when(e + slots < experts)
        def _():
            load(src, buf, e + slots).start()

    def sums_wide(t):
        def body(e, slot):
            for j in range(n):
                block = wide[slot, :, j * share : (j + 1) * share]
                part[j, t, e] = jnp.sum(jnp.abs(block), axis=0, keepdims=True)

        return body

    def sums_tall(e, slot):
        for j in range(n):
            block = tall[slot, j * share : (j + 1) * share, :]
            part[j, 2, e] = jnp.sum(jnp.abs(block).T, axis=0, keepdims=True)

    def run(src, buf, body):
        fill(src, buf)

        @pl.loop(0, experts)
        def _(e):
            take(src, buf, e, body)

    run(gate, wide, sums_wide(0))

    pl.semaphore_wait(barrier, n - 1 + owners - 1)

    stages = (pl.ds(0, 1), pl.ds(1, 2))

    def sum_copy(stage, to, src):
        return remote(
            part.at[to, stages[stage]],
            arrived.at[src, stages[stage]],
            sum_send.at[stage, to],
            sum_recv.at[stage, src],
            rows=to,
        )

    def inv_copy(stage, to, src):
        block = inverse.at[src, stages[stage]]
        return remote(block, block, inv_send.at[stage, to], inv_recv.at[stage, src], rows=to)

    def send_sums(stage):
        for k in range(1, n):
            sum_copy(stage, peer(k), me).start()

    def send_inverse(stage):
        total = part[me, stages[stage]]
        for k in range(1, n):
            sum_copy(stage, peer(k), peer(k)).wait_recv()
            total = total + arrived[peer(k), stages[stage]]
        scale = total / (rows * n)
        out_scale[stages[stage]] = scale
        inverse[me, stages[stage]] = 1.0 / scale
        for k in range(1, n):
            inv_copy(stage, peer(k), me).start()

    def await_inverse(stage):
        for k in range(1, n):
            inv_copy(stage, peer(k), peer(k)).wait_recv()

    def row_copy(to, src):
        return remote(
            router,
            out_router.at[home, :, pl.ds(pl.multiple_of(src * rows, rows), rows)],
            row_send.at[to],
            row_recv.at[src],
            rows=to,
        )

    def col_copy(to, src):
        return remote(
            out_router.at[src], out_router.at[src], col_send.at[to], col_recv.at[src], owner=to
        )

    send_sums(0)
    fill(gate, wide)
    for k in range(1, n):
        row_copy(peer(k), me).start()
    mine = out_router.at[home, :, pl.ds(pl.multiple_of(me * rows, rows), rows)]
    own_router = pltpu.make_async_copy(router, mine, own_sem.at[0])
    own_router.start()
    send_inverse(0)
    await_inverse(0)

    def block_copy(t, g, to, src):
        some = pl.ds(g * per, per)
        span = pl.ds(pl.multiple_of(src * rows, rows), rows)
        if t < 2:
            piece = send_wide.at[t, to, some]
            dst = (out_gate, out_up)[t].at[some, span, :]
        else:
            piece = send_tall.at[to, some]
            dst = out_down.at[some, :, span]
        return remote(piece, dst, send_sem.at[t, g, to], recv_sem.at[t, g, src], rows=to)

    def own_copy(t):
        span = pl.ds(pl.multiple_of(me * rows, rows), rows)
        if t < 2:
            return pltpu.make_async_copy(
                send_wide.at[t, me], (out_gate, out_up)[t].at[:, span, :], own_sem.at[1 + t]
            )
        return pltpu.make_async_copy(send_tall.at[me], out_down.at[:, :, span], own_sem.at[1 + t])

    def send_at(t, g, d):
        for side in (1, -1):
            there = chip + side * d

            @pl.when((there >= 0) & (there < chips))
            def _():
                for c in range(CORES):
                    block_copy(t, g, there * CORES + lax.rem(core + c, CORES), me).start()

    def ready_wide(t):
        def body(e, slot):
            for j in range(n):
                block = wide[slot, :, j * share : (j + 1) * share]
                send_wide[t, j, e] = (block * inverse[j, t, e]).astype(jnp.bfloat16)

        return body

    def ready_tall(e, slot):
        for j in range(n):
            block = tall[slot, j * share : (j + 1) * share, :]
            factor = jnp.broadcast_to(inverse[j, 2, e], (rows, share)).T
            send_tall[j, e] = (block * factor).astype(jnp.bfloat16)

    def send_near(t, g):
        send_at(t, g, 1)
        for c in range(1, CORES):
            block_copy(t, g, chip * CORES + lax.rem(core + c, CORES), me).start()

    def ready(t, src, buf, body, sent):
        @pl.loop(0, groups)
        def _(g):
            @pl.loop(0, per)
            def _(i):
                take(src, buf, g * per + i, body)

            @pl.when(g < sent)
            def _():
                send_near(t, g)

        own_copy(t).start()

    early = max(1, groups - 1)
    ahead = min(2, groups)
    ready(0, gate, wide, ready_wide(0), early)
    run(up, wide, sums_wide(1))
    run(down, tall, sums_tall)
    send_sums(1)
    fill(up, wide)
    fill(down, tall)
    for g in range(early, groups):
        send_near(0, g)
    send_inverse(1)
    if chips > 2:
        for g in range(ahead):
            send_at(0, g, 2)
    await_inverse(1)
    ready(1, up, wide, ready_wide(1), groups)
    ready(2, down, tall, ready_tall, groups)

    for k in range(1, n):
        row_copy(peer(k), peer(k)).wait_recv()
    own_router.wait()
    for k in range(1, owners):
        col_copy(lax.rem(home + k, owners), home).start()

    if chips > 2:

        @pl.loop(ahead, groups)
        def _(g):
            send_at(0, g, 2)

        for t in (1, 2):

            @pl.loop(0, groups)
            def _(g):
                send_at(t, g, 2)

    @pl.loop(3, max(3, chips))
    def _(d):
        for t in range(3):

            @pl.loop(0, groups)
            def _(g):
                send_at(t, g, d)

    for k in range(1, owners):
        other = lax.rem(home + k, owners)
        col_copy(other, other).wait_recv()
        col_copy(other, home).wait_send()
    for k in range(1, n):
        for stage in range(2):
            sum_copy(stage, peer(k), me).wait_send()
            inv_copy(stage, peer(k), me).wait_send()
        row_copy(peer(k), me).wait_send()
    for t in range(3):
        own_copy(t).wait()

        @pl.loop(0, groups)
        def _(g):
            @pl.loop(1, n)
            def _(k):
                block_copy(t, g, peer(k), peer(k)).wait_recv()
                block_copy(t, g, peer(k), me).wait_send()


def local(n, owners, gate, up, down, router_weight, router_gain):
    experts, rows, width = gate.shape
    share = width // n
    per = max(1, experts // GROUPS)
    groups = experts // per
    slots = min(SLOTS, experts)
    router = (router_weight * router_gain[:, None]).T.astype(jnp.bfloat16)
    anywhere = pl.BlockSpec(memory_space=pl.ANY)
    f32, bf16 = jnp.float32, jnp.bfloat16
    dma = pltpu.SemaphoreType.DMA
    ready_gate, ready_up, ready_down, scales, columns = pl.pallas_call(
        functools.partial(exchange, n, owners),
        name="exchange",
        out_shape=(
            jax.ShapeDtypeStruct((experts, rows * n, share), bf16),
            jax.ShapeDtypeStruct((experts, rows * n, share), bf16),
            jax.ShapeDtypeStruct((experts, share, rows * n), bf16),
            jax.ShapeDtypeStruct((3, experts, 1, share), f32),
            jax.ShapeDtypeStruct((owners, router.shape[0], rows * n), bf16),
        ),
        in_specs=[anywhere] * 4,
        out_specs=(
            anywhere,
            anywhere,
            anywhere,
            pl.BlockSpec(memory_space=pltpu.VMEM),
            anywhere,
        ),
        scratch_shapes=[
            pltpu.VMEM((slots, rows, width), f32),
            pltpu.VMEM((slots, width, rows), f32),
            pltpu.VMEM((2, n, experts, rows, share), bf16),
            pltpu.VMEM((n, experts, share, rows), bf16),
            pltpu.VMEM((n, 3, experts, 1, share), f32),
            pltpu.VMEM((n, 3, experts, 1, share), f32),
            pltpu.VMEM((n, 3, experts, 1, share), f32),
            dma((2, slots)),
            dma((4,)),
            dma((2, n)),
            dma((2, n)),
            dma((2, n)),
            dma((2, n)),
            dma((n,)),
            dma((n,)),
            dma((owners,)),
            dma((owners,)),
            dma((3, groups, n)),
            dma((3, groups, n)),
        ],
        compiler_params=pltpu.CompilerParams(
            collective_id=0, has_side_effects=True, vmem_limit_bytes=58 * 1024 * 1024
        ),
    )(gate, up, down, router)
    serve_router = jnp.transpose(columns, (2, 0, 1)).reshape(rows * n, -1)
    scale_gate, scale_up, scale_down = (scales[t].reshape(experts, share) for t in range(3))
    return (ready_gate, ready_up, ready_down, scale_gate, scale_up, scale_down, serve_router)


def solution(mesh):
    return jax.shard_map(
        functools.partial(local, mesh.shape["rows"], mesh.shape["owner"]),
        mesh=mesh,
        in_specs=(
            P("owner", "rows", None),
            P("owner", "rows", None),
            P("owner", None, "rows"),
            P("rows", "owner"),
            P("rows"),
        ),
        out_specs=(
            P("owner", None, "rows"),
            P("owner", None, "rows"),
            P("owner", "rows", None),
            P("owner", "rows"),
            P("owner", "rows"),
            P("owner", "rows"),
            P(),
        ),
        check_vma=False,
    )
```

time: 740 us -> 595 us (0.80)
  Pallas kernels: 0 us -> 567 us
  waiting for transfers between devices: 364 us -> 0 us
  blocking collectives: 199 us -> 0 us
  local copies, waits for them, and re-layouts: 87.7 us -> 25.7 us
  other arithmetic: 58 us -> 1.32 us
  starting transfers between devices: 14.9 us -> 0 us
  between operations: 14.2 us -> 0.64 us
    pallas_call x0 -> x1, Pallas kernels: none -> 567 us  [local(): pl.pallas_call(functools.partial(exchange, n, owners), name='exchange', o...]
    all_to_all x3 -> x0, waiting for transfers between devices: 323 us -> none  [the longest x1 167 us: local(): lax.all_to_all(narrow_gate, 'rows', split_axis=2, concat_axis=1, tiled=True)]
    all_gather x2 -> x0, blocking collectives: 199 us -> none  [the longest x1 190 us: local(): row_router = lax.all_gather(part_router, 'rows', axis=0, tiled=True)]
    all_to_all x4 -> x0, local copies, waits for them, and re-layouts: 49.4 us -> none  [the longest x2 24.8 us: local(): lax.all_to_all(narrow_down, 'rows', split_axis=1, concat_axis=2, tiled=True)]
    psum x1 -> x0, waiting for transfers between devices: 40.7 us -> none  [local(): lax.psum((jnp.sum(jnp.abs(train_gate), axis=1), jnp.sum(jnp.abs(train_up)...]
    convert_element_type x4 -> x1, other arithmetic: 36 us -> 1.32 us  [local(): router = (router_weight * router_gain[:, None]).T.astype(jnp.bfloat16)]
    reduce_sum x2 -> x0, other arithmetic: 21.2 us -> none  [the longest x1 12.6 us: local(): jnp.sum(jnp.abs(train_up), axis=1)]
    all_to_all x3 -> x0, starting transfers between devices: 14.9 us -> none  [the longest x1 5.01 us: local(): lax.all_to_all(narrow_down, 'rows', split_axis=1, concat_axis=2, tiled=True)]
  transfers between devices with their start and end apart: 4 -> 0, of which waited for: 3 -> 0; matrix products, arithmetic and copies ran while one was open for 12% -> 0% of each run, Pallas kernels for 0% -> 0%
where the time goes in v1:
time: 595 us
  Pallas kernels  567 us (95%)
  local copies, waits for them, and re-layouts  25.7 us (4%)
    pallas_call x1, Pallas kernels, local(): pl.pallas_call(functools.partial(exchange, n, owners), name='exchange', o...  567 us
    unnamed x6, local copies, waits for them, and re-layouts  24.4 us

profile of v1, /device:TPU:0, one launch (start us, length us, event | category | flops | bytes accessed | tf_op | source)
XLA Modules:
  0.0 595.0 jit_solution(14256768373469901661)
XLA Ops:
  0.6 1.3 fusion.router
  2.0 567.4 %exchange.1 = (bf16[16,2048,128]{2,1,0:T(8,128)(2,1)}, bf16[16,2048,128]{2,1,0:T(8,128)(2,1)}, bf16[16,128,2048]{2,1,0:T(8,128)(2,1)}, f32[3,16,1,128]{3,2,1,0:T(1,128)}, bf16[4,16,2048]{2,1,0:T(8,128)(2,1)}) custom-call(f32[16,256,1024]{2,1,0:T(8,128)} %gate.1, f32[16,256,1024]{2,1,0:T(8,128)} %up.1, f32[16,1024,256]{2,1,0:T(8,128)} %down.1, ...), custom_call_target="tpu_custom_call" | custom-call | tf_op jit(solution)/shard_map/exchange/pallas_call | solution.py:313
  569.3 1.3 fusion.1
  570.7 7.6 %copy.16 = bf16[16,2048,128]{2,1,0:T(8,128)(2,1)} copy(bf16[16,2048,128]{2,1,0:T(8,128)(2,1)} %get-tuple-element.27) | data formatting | bytes 16777216
  578.3 7.6 %copy.17 = bf16[16,2048,128]{2,1,0:T(8,128)(2,1)} copy(bf16[16,2048,128]{2,1,0:T(8,128)(2,1)} %get-tuple-element.28) | data formatting | bytes 16777216
  585.8 0.0 copy-start
  585.8 8.5 %copy.18 = bf16[16,128,2048]{2,1,0:T(8,128)(2,1)} copy(bf16[16,128,2048]{2,1,0:T(8,128)(2,1)} %get-tuple-element.29) | data formatting | bytes 16777216
  594.3 0.0 copy-done
  594.3 0.7 copy.19
Async XLA Ops:
  585.8 8.5 %copy-start = (bf16[4,16,2048]{2,1,0:T(8,128)(2,1)S(1)}, bf16[4,16,2048]{2,1,0:T(8,128)(2,1)}, u32[]{:S(2)}) copy-start(bf16[4,16,2048]{2,1,0:T(8,128)(2,1)} %get-tuple-element.16) | copy-start | bytes 786436
